TPU v7x, 256 devices: a whole 4x4x8 slice. The times are simulated.
256 devices in a mesh: row: 4 (over z_hi, core), col: 64 (over x, y, z_lo).
Axes of the slice: x: 4, y: 4, z: 8 (z_hi: 2, z_lo: 4; z = z_hi * 4 + z_lo), core: 2. Of those that a mesh axis runs over, the one named last changes fastest.
Arguments:
- pre_act: bfloat16 [24576, 4096], P('col'), may hold values from -16 to 16
- grad_out: bfloat16 [24576, 4096], P('col', 'row'), may hold values from -6 to 6
- w_down: bfloat16 [4096, 4096], P('col', 'row'), may hold values from -0.09375 to 0.09375
Outputs:
- w_grad: float32 [4096, 4096], P('col', 'row')
- grad_pre: bfloat16 [24576, 4096], P('col', 'row')
All inputs are finite; a program needn't handle non-finite values.
Results may differ from a plain program's by a relative error of at most 0.0095.
Values may be sent and summed in bfloat16 or wider, within the bound.
A program may use at most 128 MiB of HBM per device.

v0:
```python
import jax
import jax.numpy as jnp
from jax import lax
from jax.sharding import Mesh
from jax.sharding import PartitionSpec as P

COL = ("col_0", "col_1", "col_2")


def summed_rows(subtotal, axes):
    for axis in axes:
        subtotal = lax.psum_scatter(subtotal, axis, scatter_dimension=0, tiled=True)
    return subtotal


def per_device(pre_act, grad_out, w_down):
    hidden = jnp.maximum(pre_act, jnp.zeros((), jnp.bfloat16))
    col_count = lax.axis_size(COL)
    row_count = lax.axis_size("row")
    scale = 1.0 / jnp.sqrt(jnp.float32(hidden.shape[0] * col_count))
    quarter = hidden.shape[1] // row_count
    partial_sum = lax.dot_general(
        grad_out,
        lax.all_gather(w_down, COL, axis=0, tiled=True),
        (((1,), (1,)), ((), ())),
        preferred_element_type=jnp.float32,
    )
    term = lax.dot_general(
        hidden, grad_out, (((0,), (0,)), ((), ())), preferred_element_type=jnp.float32
    )
    w_grad = summed_rows(term * scale, COL)
    own_sum = lax.psum_scatter(
        partial_sum.astype(jnp.bfloat16), "row", scatter_dimension=1, tiled=True
    ).astype(jnp.float32)
    offset_pre = lax.axis_index("row") * quarter
    own_pre = lax.dynamic_slice_in_dim(pre_act, offset_pre, quarter, 1)
    grad_pre = jnp.where(own_pre > 0, own_sum, jnp.zeros((), jnp.float32)).astype(jnp.bfloat16)
    return (w_grad, grad_pre)


def solution(mesh):
    torus = Mesh(
        mesh.devices.reshape(mesh.shape["row"], 4, 4, 4), ("row", "col_0", "col_1", "col_2")
    )
    placed = (P(COL, None), P(COL, "row"), P(COL, "row"))
    return jax.shard_map(
        per_device,
        mesh=torus,
        in_specs=placed,
        out_specs=(P(COL, "row"), P(COL, "row")),
        check_vma=False,
    )
```

profile of v0, /device:TPU:1, one launch (start us, length us, event | category | flops | bytes accessed | tf_op | source)
XLA Modules:
  0.0 517.6 jit_solution(3365251138714423770)
XLA Ops:
  8.0 0.0 copy-start
  8.0 0.0 reduce-scatter.5.cloned.1.call-start
  8.1 1.1 copy-done
  9.1 10.0 %convolution_multiply_fusion = f32[4096,1024]{1,0:T(8,128)} fusion(bf16[384,1024]{1,0:T(8,128)(2,1)S(1)} %copy-done, bf16[384,4096]{1,0:T(8,128)(2,1)} %param.3), kind=kOutput, calls=%fused_computation | convolution fusion | flops 3226992640 | bytes 20709376 | tf_op jit(solution)/shard_map/dot_general | solution.py:28
  19.2 0.0 reduce-scatter.5.cloned.1.call-update
  19.2 0.0 all-gather.2.cloned.1.call-start
  19.2 0.5 all-gather.2.cloned.1.call-update
  19.8 0.0 reduce-scatter.7.cloned.1.call-start
  19.8 153.7 %reduce-scatter.5.cloned.1.call-done = f32[1024,1024]{1,0:T(8,128)} async-done(((f32[4096,1024]{1,0:T(8,128)}), f32[1024,1024]{1,0:T(8,128)}) %reduce-scatter.5.cloned.1.call-update) | async-done | bytes 4194320 | tf_op jit(solution)/shard_map/reduce_scatter | solution.py:12
  173.5 0.0 reduce-scatter.7.cloned.1.call-update
  173.6 0.0 reduce-scatter.11.cloned.1.call-start
  173.6 186.3 %all-gather.2.cloned.1.call-done = bf16[4096,1024]{1,0:T(8,128)(2,1)} async-done(((bf16[64,1024]{1,0:T(8,128)(2,1)}), bf16[4096,1024]{1,0:T(8,128)(2,1)}) %all-gather.2.cloned.1.call-update) | async-done | bytes 8388624 | tf_op jit(solution)/shard_map/all_gather | solution.py:24
  359.9 10.3 %convolution_convert_fusion = bf16[384,4096]{1,0:T(8,128)(2,1)} fusion(bf16[384,1024]{1,0:T(8,128)(2,1)S(1)} %copy-done, bf16[4096,1024]{1,0:T(8,128)(2,1)} %all-gather.2.cloned.1.call-done), kind=kOutput, calls=%fused_computation.1 | convolution fusion | flops 3222798336 | bytes 12320768 | tf_op jit(solution)/shard_map/dot_general | solution.py:22
  370.3 0.0 reduce-scatter.11.cloned.1.call-update
  370.3 0.0 reduce-scatter.9.cloned.1.call-start
  370.3 0.0 reduce-scatter.7.cloned.1.call-done
  370.4 0.5 reduce-scatter.9.cloned.1.call-update
  370.9 108.1 %reduce-scatter.11.cloned.1.call-done = bf16[384,1024]{1,0:T(8,128)(2,1)} async-done(((bf16[384,4096]{1,0:T(8,128)(2,1)}), bf16[384,1024]{1,0:T(8,128)(2,1)}) %reduce-scatter.11.cloned.1.call-update) | async-done | bytes 786448 | tf_op jit(solution)/shard_map/reduce_scatter | solution.py:32
  479.0 2.5 select_convert_fusion
  481.5 28.9 %reduce-scatter.9.cloned.1.call-done = f32[64,1024]{1,0:T(8,128)} async-done(((f32[256,1024]{1,0:T(8,128)}), f32[64,1024]{1,0:T(8,128)}) %reduce-scatter.9.cloned.1.call-update) | async-done | bytes 262160 | tf_op jit(solution)/shard_map/reduce_scatter | solution.py:12
Async XLA Ops:
  8.0 1.1 copy-start
  8.0 165.5 %reduce-scatter.5.cloned.1.call-start = ((), (), s32[]{:S(2)}) async-start(), calls=%async_computation.4 | async-start | bytes 20971520 | tf_op jit(solution)/shard_map/reduce_scatter | solution.py:12
  19.2 340.7 %all-gather.2.cloned.1.call-start = ((), (), s32[]{:S(2)}) async-start(), calls=%async_computation.7 | async-start | bytes 8519680 | tf_op jit(solution)/shard_map/all_gather | solution.py:24
  19.8 350.6 %reduce-scatter.7.cloned.1.call-start = ((), (), s32[]{:S(2)}) async-start(), calls=%async_computation.5 | async-start | bytes 5242880 | tf_op jit(solution)/shard_map/reduce_scatter | solution.py:12
  173.6 305.4 %reduce-scatter.11.cloned.1.call-start = ((), (), s32[]{:S(2)}) async-start(), calls=%async_computation.8 | async-start | bytes 3932160 | tf_op jit(solution)/shard_map/reduce_scatter | solution.py:32
  370.3 140.2 %reduce-scatter.9.cloned.1.call-start = ((), (), s32[]{:S(2)}) async-start(), calls=%async_computation.6 | async-start | bytes 1310720 | tf_op jit(solution)/shard_map/reduce_scatter | solution.py:12
Sparse Core Ops, SparseCore 0:
  19.3 154.1 reduce-scatter.4
  176.1 113.8 reduce-scatter.6
  370.4 108.5 reduce-scatter.10
  482.0 28.4 reduce-scatter.8
Sparse Core Ops, SparseCore 1:
  21.5 338.4 all-gather.1
where the time goes:
time: 518 us
  waiting for transfers between devices  478 us (92%)
  matrix products  20.4 us (4%)
  between operations  15.2 us (3%)
    all_gather x1, waiting for transfers between devices, per_device(): lax.all_gather(w_down, COL, axis=0, tiled=True)  186 us
    reduce_scatter x3, waiting for transfers between devices, summed_rows(): subtotal = lax.psum_scatter(subtotal, axis, scatter_dimension=0, tiled=True)  183 us
    reduce_scatter x1, waiting for transfers between devices, per_device(): lax.psum_scatter(partial_sum.astype(jnp.bfloat16), 'row', scatter_dimensi...  108 us
  transfers between devices with their start and end apart: 5, of which 4 were waited for; matrix products, arithmetic and copies ran while one was open for 2% of the time, Pallas kernels for 0%

commit v1 on v0

--- a/solution.py
+++ b/solution.py
@@ -21,7 +21,9 @@
     quarter = hidden.shape[1] // row_count
     partial_sum = lax.dot_general(
         grad_out,
-        lax.all_gather(w_down, COL, axis=0, tiled=True),
+        jnp.concatenate(
+            lax.all_to_all(jnp.stack([w_down] * lax.axis_size(COL)), COL, 0, 0), axis=0
+        ),
         (((1,), (1,)), ((), ())),
         preferred_element_type=jnp.float32,
     )

time: 518 us -> 436 us (0.84)
  waiting for transfers between devices: 478 us -> 380 us
  starting transfers between devices: 0.2 us -> 13 us
    all_gather x1 -> x0, waiting for transfers between devices: 186 us -> none  [per_device(): lax.all_gather(w_down, COL, axis=0, tiled=True)]
    reduce_scatter x3, waiting for transfers between devices: 183 us -> 308 us  [summed_rows(): subtotal = lax.psum_scatter(subtotal, axis, scatter_dimension=0, tiled=True)]
    reduce_scatter x1, waiting for transfers between devices: 108 us -> 72 us  [per_device(): lax.psum_scatter(partial_sum.astype(jnp.bfloat16), 'row', scatter_dimensi...]
    all_to_all x0 -> x1, starting transfers between devices: none -> 12.8 us  [per_device(): lax.all_to_all(jnp.stack([w_down] * lax.axis_size(COL)), COL, 0, 0)]
  transfers between devices with their start and end apart: 5 -> 5, of which waited for: 4 -> 4; matrix products, arithmetic and copies ran while one was open for 2% -> 4% of each run, Pallas kernels for 0% -> 0%
where the time goes in v1:
time: 436 us; the launch traced here: 435 us
  waiting for transfers between devices  380 us (87%)
  matrix products  20.4 us (5%)
  between operations  13.8 us (3%)
  starting transfers between devices  13 us (3%)
  local copies, waits for them, and re-layouts  6.24 us (1%)
    reduce_scatter x3, waiting for transfers between devices, summed_rows(): subtotal = lax.psum_scatter(subtotal, axis, scatter_dimension=0, tiled=True)  308 us
    reduce_scatter x1, waiting for transfers between devices, per_device(): lax.psum_scatter(partial_sum.astype(jnp.bfloat16), 'row', scatter_dimensi...  72 us
    all_to_all x1, starting transfers between devices, per_device(): lax.all_to_all(jnp.stack([w_down] * lax.axis_size(COL)), COL, 0, 0)  12.8 us
    dot_general x1, matrix products, per_device(): lax.dot_general(grad_out, jnp.concatenate(lax.all_to_all(jnp.stack([w_dow...  10.3 us
    dot_general x1, matrix products, per_device(): lax.dot_general(hidden, grad_out, (((0,), (0,)), ((), ())), preferred_ele...  10 us
  transfers between devices with their start and end apart: 5, of which 4 were waited for; matrix products, arithmetic and copies ran while one was open for 4% of the time, Pallas kernels for 0%

profile of v1, /device:TPU:1, one launch (start us, length us, event | category | flops | bytes accessed | tf_op | source)
XLA Modules:
  0.0 435.4 jit_solution(3062430325637846897)
XLA Ops:
  7.2 0.0 copy-start
  7.2 0.0 reduce-scatter.5.cloned.1.call-start
  7.2 1.1 copy-done
  8.3 10.0 %convolution_multiply_fusion = f32[4096,1024]{1,0:T(8,128)} fusion(bf16[384,1024]{1,0:T(8,128)(2,1)S(1)} %copy-done, bf16[384,4096]{1,0:T(8,128)(2,1)} %param.3), kind=kOutput, calls=%fused_computation | convolution fusion | flops 3226992640 | bytes 20709376 | tf_op jit(solution)/shard_map/dot_general | solution.py:30
  18.3 0.0 copy-start.1
  18.3 0.0 reduce-scatter.5.cloned.1.call-update
  18.4 0.9 copy-done.1
  19.2 4.3 stack.2
  23.5 12.8 %all-to-all-start = ((bf16[64,64,1024]{2,1,0:T(8,128)(2,1)}), bf16[64,64,1024]{2,1,0:T(8,128)(2,1)}, u32[]{:S(2)}, u32[]{:S(2)}) async-start(bf16[64,64,1024]{2,1,0:T(8,128)(2,1)} %stack.2), calls=%async_computation.3 | async-start | bytes 16777216 | tf_op jit(solution)/shard_map/all_to_all | solution.py:25
  36.3 0.0 reduce-scatter.7.cloned.1.call-start
  36.4 226.3 %reduce-scatter.5.cloned.1.call-done = f32[1024,1024]{1,0:T(8,128)} async-done(((f32[4096,1024]{1,0:T(8,128)}), f32[1024,1024]{1,0:T(8,128)}) %reduce-scatter.5.cloned.1.call-update) | async-done | bytes 4194320 | tf_op jit(solution)/shard_map/reduce_scatter | solution.py:12
  262.7 0.0 reduce-scatter.7.cloned.1.call-update
  262.7 0.0 reduce-scatter.11.cloned.1.call-start
  262.8 0.0 all-to-all-done
  262.8 10.3 %convolution_convert_fusion = bf16[384,4096]{1,0:T(8,128)(2,1)} fusion(bf16[384,1024]{1,0:T(8,128)(2,1)S(1)} %copy-done, bf16[4096,1024]{1,0:T(8,128)(2,1)} %bitcast), kind=kOutput, calls=%fused_computation.1 | convolution fusion | flops 3222798336 | bytes 12320768 | tf_op jit(solution)/shard_map/dot_general | solution.py:22
  273.1 0.0 reduce-scatter.11.cloned.1.call-update
  273.2 0.0 reduce-scatter.9.cloned.1.call-start
  273.2 52.3 %reduce-scatter.7.cloned.1.call-done = f32[256,1024]{1,0:T(8,128)} async-done(((f32[1024,1024]{1,0:T(8,128)}), f32[256,1024]{1,0:T(8,128)}) %reduce-scatter.7.cloned.1.call-update) | async-done | bytes 1048592 | tf_op jit(solution)/shard_map/reduce_scatter | solution.py:12
  325.5 0.0 reduce-scatter.9.cloned.1.call-update
  325.5 72.0 %reduce-scatter.11.cloned.1.call-done = bf16[384,1024]{1,0:T(8,128)(2,1)} async-done(((bf16[384,4096]{1,0:T(8,128)(2,1)}), bf16[384,1024]{1,0:T(8,128)(2,1)}) %reduce-scatter.11.cloned.1.call-update) | async-done | bytes 786448 | tf_op jit(solution)/shard_map/reduce_scatter | solution.py:34
  397.4 2.5 select_convert_fusion
  400.0 28.9 %reduce-scatter.9.cloned.1.call-done = f32[64,1024]{1,0:T(8,128)} async-done(((f32[256,1024]{1,0:T(8,128)}), f32[64,1024]{1,0:T(8,128)}) %reduce-scatter.9.cloned.1.call-update) | async-done | bytes 262160 | tf_op jit(solution)/shard_map/reduce_scatter | solution.py:12
Async XLA Ops:
  7.2 1.1 copy-start
  7.2 255.5 %reduce-scatter.5.cloned.1.call-start = ((), (), s32[]{:S(2)}) async-start(), calls=%async_computation.5 | async-start | bytes 20971520 | tf_op jit(solution)/shard_map/reduce_scatter | solution.py:12
  18.3 0.9 copy-start.1
  23.5 239.3 %all-to-all-start = ((bf16[64,64,1024]{2,1,0:T(8,128)(2,1)}), bf16[64,64,1024]{2,1,0:T(8,128)(2,1)}, u32[]{:S(2)}, u32[]{:S(2)}) async-start(bf16[64,64,1024]{2,1,0:T(8,128)(2,1)} %stack.2), calls=%async_computation.3 | async-start | bytes 16777216 | tf_op jit(solution)/shard_map/all_to_all | solution.py:25
  36.3 289.1 %reduce-scatter.7.cloned.1.call-start = ((), (), s32[]{:S(2)}) async-start(), calls=%async_computation.6 | async-start | bytes 5242880 | tf_op jit(solution)/shard_map/reduce_scatter | solution.py:12
  262.7 134.7 %reduce-scatter.11.cloned.1.call-start = ((), (), s32[]{:S(2)}) async-start(), calls=%async_computation.8 | async-start | bytes 3932160 | tf_op jit(solution)/shard_map/reduce_scatter | solution.py:34
  273.2 155.8 %reduce-scatter.9.cloned.1.call-start = ((), (), s32[]{:S(2)}) async-start(), calls=%async_computation.7 | async-start | bytes 1310720 | tf_op jit(solution)/shard_map/reduce_scatter | solution.py:12
Sparse Core Ops, SparseCore 0:
  18.5 244.1 reduce-scatter.4
  265.3 60.1 reduce-scatter.6
  328.2 69.1 reduce-scatter.10
  400.4 28.4 reduce-scatter.8
